TPU v7x, 32 devices: a whole 2x2x4 slice. The times are simulated.
32 devices in a mesh: dom: 32 (over z, y, x, core).
Axes of the slice: x: 2, y: 2, z: 4, core: 2. Of those that a mesh axis runs over, the one named last changes fastest.
Arguments:
- forcing: float32 [1024, 128], P('dom'), may hold values from -6 to 6
- first_guess: float32 [1024, 128], P('dom'), may hold values from -4 to 4
- corners: int32 [3, 262144], P(None, 'dom'), may hold values from 0 to 8191, as said below
- gradients: float32 [4, 262144], P(None, 'dom'), may hold values from -5 to 5
- element_area: float32 [262144], P('dom'), may hold values from 0.5 to 2
- element_depth: float32 [262144], P('dom'), may hold values from 0.2 to 4
- send_blocks: int32 [32, 4, 8], P('dom'), may hold values from 0 to 32, as said below
- recv_blocks: int32 [32, 4, 8], P('dom'), may hold values from 0 to 32, as said below
Outputs:
- elevation: float32 [1024, 128], P('dom')
- residual_left: float32 [1024, 128], P('dom')
Inputs may be any that keep to these rules, and one draw needn't show every extreme that they name: `corners`: column e of device d's elements names three different local nodes of device d, numbered below (64) * 128: numbers below 4096 are its owned nodes in block order, the rest its halo blocks. The first corner is an owned node, and every owned node is the first corner of some element of its device. `send_blocks`: entry [d, o, s] is the owned block of device d sent in slot s of offset o to the reader d - k_o, or 32 for an empty slot; it is live exactly when recv_blocks[d - k_o, o, s] is, and readers outside the mesh get nothing. Live blocks of one device and offset differ. For k_o = 1 every slot toward an existing reader is live. `recv_blocks`: entry [q, o, s] is the halo block of device q filled by slot s of offset o from device q + k_o, or 32 for an empty slot. The live entries of one device differ.
All inputs are finite; a program needn't handle non-finite values.
Results may differ from a plain program's by a relative error of at most 0.00022.
Values sent between devices are 32-bit elements; how exact they have to be, the bound alone decides.
A program may use at most 64 MiB of HBM per device.

v0:
```python
import jax
import jax.numpy as jnp
from jax import lax
from jax.sharding import PartitionSpec as P

ITERS = 2


def passed_along(block, axis, distance):
    devices = range(lax.axis_size(axis))
    route = [(i - distance, i) for i in devices if i - distance in devices]
    return lax.ppermute(block, axis, route)


def shift_list(offsets):
    half_count = offsets // 2
    return [
        shift_at - half_count if shift_at < half_count else shift_at - half_count + 1
        for shift_at in range(offsets)
    ]


def onehot_mul(left, right):
    return jnp.dot(left, right, precision=lax.Precision.HIGHEST, preferred_element_type=jnp.float32)


def local(
    forcing, first_guess, corners, gradients, element_area, element_depth, send_blocks, recv_blocks
):
    own_count, columns = forcing.shape
    offsets = send_blocks.shape[1]
    slot_count = send_blocks.shape[2]
    halo_count = offsets * slot_count
    all_blocks = own_count + halo_count
    local_total = all_blocks * columns
    shifts = shift_list(offsets)
    send_hot = (
        send_blocks.reshape(-1)[:, None] == jnp.arange(own_count, dtype=jnp.int32)[None, :]
    ).astype(jnp.float32)
    recv_hot = (
        jnp.arange(halo_count, dtype=jnp.int32)[:, None] == recv_blocks.reshape(-1)[None, :]
    ).astype(jnp.float32)

    def forward(owned_vals):
        outgoing = onehot_mul(send_hot, owned_vals).reshape(offsets, slot_count, columns)
        pieces = []
        for position in range(offsets):
            pieces.append(passed_along(outgoing[position], "dom", -shifts[position]))
        incoming = jnp.stack(pieces)
        return onehot_mul(recv_hot, incoming.reshape(halo_count, columns))

    def backward(halo_part):
        outgoing = onehot_mul(recv_hot.T, halo_part).reshape(offsets, slot_count, columns)
        pieces = []
        for position in range(offsets):
            pieces.append(passed_along(outgoing[position], "dom", shifts[position]))
        incoming = jnp.stack(pieces)
        return onehot_mul(send_hot.T, incoming.reshape(halo_count, columns))

    grad_x = [gradients[0], gradients[2], -(gradients[0] + gradients[2])]
    grad_y = [gradients[1], gradients[3], -(gradients[1] + gradients[3])]
    scaled = element_depth * element_area
    stiffness = [
        [
            scaled * (grad_x[row_at] * grad_x[col_at] + grad_y[row_at] * grad_y[col_at])
            for col_at in range(3)
        ]
        for row_at in range(3)
    ]
    flat_corners = corners.reshape(-1)
    third = element_area / 3.0
    mass_local = jax.ops.segment_sum(
        jnp.concatenate([third, third, third]), flat_corners, num_segments=local_total
    ).reshape(all_blocks, columns)
    mass = mass_local[:own_count] + backward(mass_local[own_count:])

    def operate(field):
        local_vals = jnp.concatenate([field, forward(field)], axis=0).reshape(-1)
        values = [jnp.take(local_vals, corners[corner_at], axis=0) for corner_at in range(3)]
        contrib = jnp.concatenate(
            [
                stiffness[row_at][0] * values[0]
                + stiffness[row_at][1] * values[1]
                + stiffness[row_at][2] * values[2]
                for row_at in range(3)
            ]
        )
        summed = jax.ops.segment_sum(contrib, flat_corners, num_segments=local_total).reshape(
            all_blocks, columns
        )
        return mass * field + summed[:own_count] + backward(summed[own_count:])

    def paired(vector, applied):
        return lax.psum((jnp.sum(vector * vector), jnp.sum(vector * applied)), "dom")

    elevation = first_guess
    residual = forcing - operate(first_guess)
    applied = operate(residual)
    norm_now, crossed = paired(residual, applied)
    step_size = norm_now / crossed
    direction = residual
    search_image = applied
    for step_at in range(ITERS):
        elevation = elevation + step_size * direction
        residual = residual - step_size * search_image
        if step_at + 1 < ITERS:
            applied = operate(residual)
            norm_next, crossed = paired(residual, applied)
            beta_ratio = norm_next / norm_now
            step_size = norm_next / (crossed - beta_ratio * norm_next / step_size)
            direction = residual + beta_ratio * direction
            search_image = applied + beta_ratio * search_image
            norm_now = norm_next
    return (elevation, residual)


def solution(mesh):
    placed = (
        P("dom", None),
        P("dom", None),
        P(None, "dom"),
        P(None, "dom"),
        P("dom"),
        P("dom"),
        P("dom", None, None),
        P("dom", None, None),
    )
    return jax.shard_map(
        local,
        mesh=mesh,
        in_specs=placed,
        out_specs=(P("dom", None), P("dom", None)),
        check_vma=False,
    )
```

profile of v0, /device:TPU:0, one launch (start us, length us, event | category | flops | bytes accessed | tf_op | source)
XLA Modules:
  0.0 1125.4 jit_solution(6838695664793218546)
XLA Ops:
  2.3 4.9 collective-permute-start.4
  16.6 45.5 %gather_fusion.2 = f32[8192]{0:T(1024)S(1)} fusion(f32[8192]{0:T(1024)S(1)} %maximum_bitcast_fusion, s32[8192]{0:T(1024)S(1)} %fusion.3), kind=kCustom, calls=%fused_computation.2.clone | custom fusion | bytes 98304 | tf_op jit(solution)/shard_map/jit(_take)/gather | solution.py:79
  62.1 45.5 %gather_fusion = f32[8192]{0:T(1024)S(1)} fusion(f32[8192]{0:T(1024)S(1)} %maximum_bitcast_fusion, s32[8192]{0:T(1024)S(1)} %fusion.1), kind=kCustom, calls=%fused_computation.clone | custom fusion | bytes 98304 | tf_op jit(solution)/shard_map/jit(_take)/gather | solution.py:79
  107.7 45.5 %gather_fusion.1 = f32[8192]{0:T(1024)S(1)} fusion(f32[8192]{0:T(1024)S(1)} %maximum_bitcast_fusion, s32[8192]{0:T(1024)S(1)} %fusion.2), kind=kCustom, calls=%fused_computation.1.clone | custom fusion | bytes 98304 | tf_op jit(solution)/shard_map/jit(_take)/gather | solution.py:79
  153.3 128.5 %scatter_custom_fusion = f32[8192]{0:T(1024)S(1)} fusion(s32[24576]{0:T(1024)S(1)} %reshape.264, f32[24576]{0:T(1024)S(1)} %pad_maximum_fusion, f32[]{:T(128)} %constant.2.clone.1), kind=kCustom, calls=%fused_computation.135 | custom fusion | flops 24576 | bytes 32772 | tf_op jit(solution)/shard_map/scatter-add | solution.py:72
  283.3 5.2 collective-permute-start.3
  293.6 128.5 %scatter_custom_fusion.1 = f32[8192]{0:T(1024)S(1)} fusion(s32[24576]{0:T(1024)S(1)} %reshape.264, f32[24576]{0:T(1024)S(1)} %pad_maximum_fusion.1, f32[]{:T(128)} %constant.2.clone.1), kind=kCustom, calls=%fused_computation.133 | custom fusion | flops 24576 | bytes 32772 | tf_op jit(solution)/shard_map/scatter-add | solution.py:88
  423.5 6.1 collective-permute-start.11
  437.7 4.2 collective-permute-start.12
  444.5 5.2 collective-permute-start.13
  450.7 45.5 %gather_fusion.5 = f32[8192]{0:T(1024)S(1)} fusion(f32[8192]{0:T(1024)S(1)} %maximum_bitcast_fusion.1, s32[8192]{0:T(1024)S(1)} %fusion.3), kind=kCustom, calls=%fused_computation.5.clone | custom fusion | bytes 98304 | tf_op jit(solution)/shard_map/jit(_take)/gather | solution.py:79
  496.2 45.5 %gather_fusion.4 = f32[8192]{0:T(1024)S(1)} fusion(f32[8192]{0:T(1024)S(1)} %maximum_bitcast_fusion.1, s32[8192]{0:T(1024)S(1)} %fusion.2), kind=kCustom, calls=%fused_computation.4.clone | custom fusion | bytes 98304 | tf_op jit(solution)/shard_map/jit(_take)/gather | solution.py:79
  541.7 45.5 %gather_fusion.3 = f32[8192]{0:T(1024)S(1)} fusion(f32[8192]{0:T(1024)S(1)} %maximum_bitcast_fusion.1, s32[8192]{0:T(1024)S(1)} %fusion.1), kind=kCustom, calls=%fused_computation.3.clone | custom fusion | bytes 98304 | tf_op jit(solution)/shard_map/jit(_take)/gather | solution.py:79
  587.3 128.5 %scatter_custom_fusion.2 = f32[8192]{0:T(1024)S(1)} fusion(s32[24576]{0:T(1024)S(1)} %reshape.264, f32[24576]{0:T(1024)S(1)} %pad_maximum_fusion.2, f32[]{:T(128)} %constant.2.clone.1), kind=kCustom, calls=%fused_computation.131 | custom fusion | flops 24576 | bytes 32772 | tf_op jit(solution)/shard_map/scatter-add | solution.py:88
  717.3 6.4 collective-permute-start.19
  728.8 4.7 collective-permute-done.17
  734.3 47.7 %all-reduce.1 = (f32[]{:T(128)}, f32[]{:T(128)}) all-reduce(f32[]{:T(128)} %get-tuple-element.6, f32[]{:T(128)} %get-tuple-element.5), channel_id=1, replica_groups=mesh['dom'=32] {'dom'}, use_global_device_ids=true, to_apply=%region_3.5 | all-reduce | flops 2 | bytes 16 | tf_op jit(solution)/shard_map/psum | solution.py:94
  794.4 45.5 %gather_fusion.8 = f32[8192]{0:T(1024)S(1)} fusion(f32[8192]{0:T(1024)S(1)} %maximum_bitcast_fusion.2, s32[8192]{0:T(1024)S(1)} %fusion.3), kind=kCustom, calls=%fused_computation.8.clone | custom fusion | bytes 98304 | tf_op jit(solution)/shard_map/jit(_take)/gather | solution.py:79
  839.9 45.5 %gather_fusion.7 = f32[8192]{0:T(1024)S(1)} fusion(f32[8192]{0:T(1024)S(1)} %maximum_bitcast_fusion.2, s32[8192]{0:T(1024)S(1)} %fusion.2), kind=kCustom, calls=%fused_computation.7.clone | custom fusion | bytes 98304 | tf_op jit(solution)/shard_map/jit(_take)/gather | solution.py:79
  885.4 45.5 %gather_fusion.6 = f32[8192]{0:T(1024)S(1)} fusion(f32[8192]{0:T(1024)S(1)} %maximum_bitcast_fusion.2, s32[8192]{0:T(1024)S(1)} %fusion.1), kind=kCustom, calls=%fused_computation.6.clone | custom fusion | bytes 98304 | tf_op jit(solution)/shard_map/jit(_take)/gather | solution.py:79
  931.0 128.5 %scatter_custom_fusion.3 = f32[8192]{0:T(1024)S(1)} fusion(s32[24576]{0:T(1024)S(1)} %reshape.264, f32[24576]{0:T(1024)S(1)} %pad_maximum_fusion.3, f32[]{:T(128)} %constant.2.clone.1), kind=kCustom, calls=%fused_computation.129 | custom fusion | flops 24576 | bytes 32772 | tf_op jit(solution)/shard_map/scatter-add | solution.py:88
  1061.0 6.9 collective-permute-start.27
  1071.3 4.7 collective-permute-done.25
  1076.9 43.4 %all-reduce = (f32[]{:T(128)}, f32[]{:T(128)}) all-reduce(f32[]{:T(128)} %get-tuple-element.4, f32[]{:T(128)} %get-tuple-element.3), channel_id=1, replica_groups=mesh['dom'=32] {'dom'}, use_global_device_ids=true, to_apply=%region_8.10 | all-reduce | flops 2 | bytes 16 | tf_op jit(solution)/shard_map/psum | solution.py:94
  (104 shorter events, 55.3 us)
Async XLA Ops:
  2.3 13.5 %collective-permute-start.4 = (f32[8,128]{1,0:T(8,128)S(1)}, f32[8,128]{1,0:T(8,128)S(1)}, u32[]{:S(2)}, u32[]{:S(2)}) collective-permute-start(f32[8,128]{1,0:T(8,128)S(1)} %get-tuple-element.64), channel_id=1, source_target_pairs={{0,2},{1,3},{2,4},{3,5},{4,6},{5,7},{6,8},{7,9},{8,10},{9,11},{10,... | collective-permute-start | bytes 12296 | tf_op jit(solution)/shard_map/ppermute | solution.py:12
  7.2 8.7 collective-permute-start.7
  8.5 7.4 collective-permute-start.6
  9.8 6.1 collective-permute-start.5
  282.0 141.5 %collective-permute-start = (f32[8,128]{1,0:T(8,128)S(1)}, f32[8,128]{1,0:T(8,128)S(1)}, u32[]{:S(2)}, u32[]{:S(2)}) collective-permute-start(f32[8,128]{1,0:T(8,128)S(1)} %get-tuple-element.56), channel_id=1, source_target_pairs={{2,0},{3,1},{4,2},{5,3},{6,4},{7,5},{8,6},{9,7},{10,8},{11,9},{12,... | collective-permute-start | bytes 12296 | tf_op jit(solution)/shard_map/ppermute | solution.py:12
  283.3 146.3 %collective-permute-start.3 = (f32[8,128]{1,0:T(8,128)S(1)}, f32[8,128]{1,0:T(8,128)S(1)}, u32[]{:S(2)}, u32[]{:S(2)}) collective-permute-start(f32[8,128]{1,0:T(8,128)S(1)} %get-tuple-element.57), channel_id=1, source_target_pairs={{0,2},{1,3},{2,4},{3,5},{4,6},{5,7},{6,8},{7,9},{8,10},{9,11},{10,... | collective-permute-start | bytes 12296 | tf_op jit(solution)/shard_map/ppermute | solution.py:12
  288.5 143.2 %collective-permute-start.2 = (f32[8,128]{1,0:T(8,128)S(1)}, f32[8,128]{1,0:T(8,128)S(1)}, u32[]{:S(2)}, u32[]{:S(2)}) collective-permute-start(f32[8,128]{1,0:T(8,128)S(1)} %get-tuple-element.58), channel_id=1, source_target_pairs={{0,1},{1,2},{2,3},{3,4},{4,5},{5,6},{6,7},{7,8},{8,9},{9,10},{10,1... | collective-permute-start | bytes 12296 | tf_op jit(solution)/shard_map/ppermute | solution.py:12
  292.2 140.8 %collective-permute-start.1 = (f32[8,128]{1,0:T(8,128)S(1)}, f32[8,128]{1,0:T(8,128)S(1)}, u32[]{:S(2)}, u32[]{:S(2)}) collective-permute-start(f32[8,128]{1,0:T(8,128)S(1)} %get-tuple-element.59), channel_id=1, source_target_pairs={{1,0},{2,1},{3,2},{4,3},{5,4},{6,5},{7,6},{8,7},{9,8},{10,9},{11,1... | collective-permute-start | bytes 12296 | tf_op jit(solution)/shard_map/ppermute | solution.py:12
  422.2 11.1 collective-permute-start.8
  423.5 9.8 collective-permute-start.11
  431.7 5.5 collective-permute-start.9
  437.7 12.1 %collective-permute-start.12 = (f32[8,128]{1,0:T(8,128)S(1)}, f32[8,128]{1,0:T(8,128)S(1)}, u32[]{:S(2)}, u32[]{:S(2)}) collective-permute-start(f32[8,128]{1,0:T(8,128)S(1)} %get-tuple-element.52), channel_id=1, source_target_pairs={{0,2},{1,3},{2,4},{3,5},{4,6},{5,7},{6,8},{7,9},{8,10},{9,11},{10,... | collective-permute-start | bytes 12296 | tf_op jit(solution)/shard_map/ppermute | solution.py:12
  441.9 7.9 collective-permute-start.15
  443.2 6.6 collective-permute-start.14
  444.5 6.1 collective-permute-start.13
  716.0 12.7 %collective-permute-start.16 = (f32[8,128]{1,0:T(8,128)S(1)}, f32[8,128]{1,0:T(8,128)S(1)}, u32[]{:S(2)}, u32[]{:S(2)}) collective-permute-start(f32[8,128]{1,0:T(8,128)S(1)} %get-tuple-element.48), channel_id=1, source_target_pairs={{2,0},{3,1},{4,2},{5,3},{6,4},{7,5},{8,6},{9,7},{10,8},{11,9},{12,... | collective-permute-start | bytes 12296 | tf_op jit(solution)/shard_map/ppermute | solution.py:12
  717.3 11.4 %collective-permute-start.19 = (f32[8,128]{1,0:T(8,128)S(1)}, f32[8,128]{1,0:T(8,128)S(1)}, u32[]{:S(2)}, u32[]{:S(2)}) collective-permute-start(f32[8,128]{1,0:T(8,128)S(1)} %get-tuple-element.49), channel_id=1, source_target_pairs={{0,2},{1,3},{2,4},{3,5},{4,6},{5,7},{6,8},{7,9},{8,10},{9,11},{10,... | collective-permute-start | bytes 12296 | tf_op jit(solution)/shard_map/ppermute | solution.py:12
  723.7 5.1 collective-permute-start.18
  727.4 6.0 collective-permute-start.17
  783.6 9.8 collective-permute-start.20
  787.8 5.7 collective-permute-start.23
  1059.7 11.5 %collective-permute-start.24 = (f32[8,128]{1,0:T(8,128)S(1)}, f32[8,128]{1,0:T(8,128)S(1)}, u32[]{:S(2)}, u32[]{:S(2)}) collective-permute-start(f32[8,128]{1,0:T(8,128)S(1)} %get-tuple-element.40), channel_id=1, source_target_pairs={{2,0},{3,1},{4,2},{5,3},{6,4},{7,5},{8,6},{9,7},{10,8},{11,9},{12,... | collective-permute-start | bytes 12296 | tf_op jit(solution)/shard_map/ppermute | solution.py:12
  1061.0 10.2 collective-permute-start.27
  1069.9 6.0 collective-permute-start.25
  (11 other events, 117.2 us)
where the time goes:
time: 1130 us
  other arithmetic  515 us (46%)
  local copies, waits for them, and re-layouts  414 us (37%)
  blocking collectives  91.1 us (8%)
  starting transfers between devices  78.7 us (7%)
  waiting for transfers between devices  14.9 us (1%)
    gather x9, local copies, waits for them, and re-layouts, operate(): jnp.take(local_vals, corners[corner_at], axis=0)  410 us
    scatter-add x3, other arithmetic, operate(): jax.ops.segment_sum(contrib, flat_corners, num_segments=local_total)  385 us
    scatter-add x1, other arithmetic, local(): jax.ops.segment_sum(jnp.concatenate([third, third, third]), flat_corners,...  128 us
    psum x2, blocking collectives, paired(): lax.psum((jnp.sum(vector * vector), jnp.sum(vector * applied)), 'dom')  91.1 us
    ppermute x28, starting transfers between devices, passed_along(): return lax.ppermute(block, axis, route)  78.7 us
  transfers between devices with their start and end apart: 28, of which 5 were waited for; matrix products, arithmetic and copies ran while one was open for 12% of the time, Pallas kernels for 0%

commit v1 on v0

v1 whole, which is shorter than its diff:
```python
import functools

import jax
import jax.numpy as jnp
from jax import lax
from jax.experimental import pallas as pl
from jax.experimental.pallas import tpu as pltpu
from jax.sharding import PartitionSpec as P

LANES = 128
ROWS = 8


def shift_list(offsets):
    half_count = offsets // 2
    return [
        shift_at - half_count if shift_at < half_count else shift_at - half_count + 1
        for shift_at in range(offsets)
    ]


def kernel(
    n,
    forcing,
    guess,
    corners,
    gradients,
    area,
    depth,
    send,
    recv,
    elevation,
    residual,
    blk,
    lane,
    hot,
    elem,
    vals,
    hi,
    lo,
    field,
    halo_part,
    fwd_out,
    fwd_in,
    bwd_out,
    bwd_in,
    sum_out,
    sum_in,
    fwd_send_sem,
    fwd_recv_sem,
    bwd_send_sem,
    bwd_recv_sem,
    sum_send_sem,
    sum_recv_sem,
):
    own, _ = forcing.shape
    _, offsets, slots = send.shape
    halo = offsets * slots
    rows = area.shape[0]
    groups = rows // ROWS
    shifts = shift_list(offsets)
    me = lax.axis_index("dom")
    f32 = jnp.float32

    barrier = pltpu.get_barrier_semaphore()

    def greet(i, carry):
        pl.semaphore_signal(
            barrier, inc=1, device_id=(lax.rem(me + i, n),), device_id_type=pl.DeviceIdType.MESH
        )
        return carry

    lax.fori_loop(1, n, greet, 0)

    def there(distance):
        return jnp.logical_and(me + distance >= 0, me + distance < n)

    def fwd_copy(t, o):
        return pltpu.make_async_remote_copy(
            src_ref=fwd_out.at[t, o],
            dst_ref=fwd_in.at[t, o],
            send_sem=fwd_send_sem.at[t, o],
            recv_sem=fwd_recv_sem.at[t, o],
            device_id=(me - shifts[o],),
            device_id_type=pl.DeviceIdType.MESH,
        )

    def bwd_copy(t, o):
        return pltpu.make_async_remote_copy(
            src_ref=bwd_out.at[t, o],
            dst_ref=bwd_in.at[t, o],
            send_sem=bwd_send_sem.at[t, o],
            recv_sem=bwd_recv_sem.at[t, o],
            device_id=(me + shifts[o],),
            device_id_type=pl.DeviceIdType.MESH,
        )

    def when_there(distance, action):
        @pl.when(there(distance))
        def _():
            action()

    for o in range(offsets):

        @pl.when(jnp.logical_not(there(shifts[o])))
        def _():
            for t in range(3):
                fwd_in[t, o] = jnp.zeros((slots, LANES), f32)

        @pl.when(jnp.logical_not(there(-shifts[o])))
        def _():
            for t in range(3):
                bwd_in[t, o] = jnp.zeros((slots, LANES), f32)

    def pack(t, source):
        for o in range(offsets):
            for s in range(slots):
                at = jnp.minimum(send[0, o, s], own - 1)
                fwd_out[t, o, s : s + 1, :] = source[pl.ds(at, 1), :]

    def start_forward(t):
        for o in range(offsets):
            when_there(-shifts[o], lambda o=o: fwd_copy(t, o).start())

    pack(0, guess)
    pl.semaphore_wait(barrier, n - 1)
    start_forward(0)

    def lay(r, carry):
        at = pl.multiple_of(r * LANES, LANES)
        for c in range(3):
            lane[pl.ds(c * rows + r, 1), :] = corners[c : c + 1, pl.ds(at, LANES)]
        for c in range(4):
            elem[pl.ds(c * rows + r, 1), :] = gradients[c : c + 1, pl.ds(at, LANES)]
        return carry

    lax.fori_loop(0, rows, lay, 0)

    wide = lax.broadcasted_iota(jnp.int32, (ROWS, LANES), 1)
    table = jnp.where(wide < own, wide, 2 * LANES)
    for o in range(offsets):
        for s in range(slots):
            table = jnp.where(wide == own + recv[0, o, s], own + o * slots + s, table)
    table = jnp.where(wide < own + halo, table, 2 * LANES)

    def number(g, carry):
        at = pl.multiple_of(g * ROWS, ROWS)
        node = lane[pl.ds(at, ROWS), :]
        block = lax.shift_right_logical(node, 7)
        blk[pl.ds(at, ROWS), :] = jnp.take_along_axis(
            table, block, axis=1, mode="promise_in_bounds"
        )
        lane[pl.ds(at, ROWS), :] = lax.bitwise_and(node, LANES - 1)
        return carry

    lax.fori_loop(0, 3 * groups, number, 0)

    tall = lax.broadcasted_iota(jnp.int32, (LANES, LANES), 0)

    def heat(g, carry):
        at = pl.multiple_of(g * ROWS, ROWS)
        for j in range(ROWS):
            row = lane[pl.ds(at + j, 1), :]
            hot[:, pl.ds(pl.multiple_of((at + j) * LANES, LANES), LANES)] = jnp.where(
                row == tall, 1.0, 0.0
            ).astype(jnp.bfloat16)
        return carry

    lax.fori_loop(0, 3 * groups, heat, 0)

    def picked(source, count, first, value, index, block):
        for b in range(count):
            row = jnp.broadcast_to(source(b), (ROWS, LANES))
            got = jnp.take_along_axis(row, index, axis=1, mode="promise_in_bounds")
            value = jnp.where(block == first + b, got, value)
        return value

    def operate(t, source):
        def gather_own(g, carry):
            at = pl.multiple_of(g * ROWS, ROWS)
            index = lane[pl.ds(at, ROWS), :]
            block = blk[pl.ds(at, ROWS), :]
            vals[pl.ds(at, ROWS), :] = picked(
                lambda b: source[b : b + 1, :],
                own,
                0,
                jnp.zeros((ROWS, LANES), f32),
                index,
                block,
            )
            return carry

        lax.fori_loop(0, 3 * groups, gather_own, 0)

        for o in range(offsets):
            when_there(shifts[o], lambda o=o: fwd_copy(t, o).wait_recv())

        def gather_halo(g, carry):
            at = pl.multiple_of(g * ROWS, ROWS)
            u = [vals[pl.ds(at, ROWS), :]]
            for c in (1, 2):
                here = pl.multiple_of(c * rows + at, ROWS)
                u.append(
                    picked(
                        lambda b: fwd_in[t, b // slots, b % slots : b % slots + 1, :],
                        halo,
                        own,
                        vals[pl.ds(here, ROWS), :],
                        lane[pl.ds(here, ROWS), :],
                        blk[pl.ds(here, ROWS), :],
                    )
                )
            gx0, gy0, gx1, gy1 = [
                elem[pl.ds(pl.multiple_of(c * rows + at, ROWS), ROWS), :] for c in range(4)
            ]
            size = area[pl.ds(at, ROWS), :]
            scaled = depth[pl.ds(at, ROWS), :] * size
            third = size / 3.0
            from0, from1 = u[0] - u[2], u[1] - u[2]
            slope_x = scaled * (gx0 * from0 + gx1 * from1)
            slope_y = scaled * (gy0 * from0 + gy1 * from1)
            flow0 = gx0 * slope_x + gy0 * slope_y
            flow1 = gx1 * slope_x + gy1 * slope_y
            adds = [
                flow0 + third * u[0],
                flow1 + third * u[1],
                third * u[2] - (flow0 + flow1),
            ]
            for c in range(3):
                here = pl.multiple_of(c * rows + at, ROWS)
                top = adds[c].astype(jnp.bfloat16).astype(f32)
                hi[pl.ds(here, ROWS), :] = top
                lo[pl.ds(here, ROWS), :] = adds[c] - top
            return carry

        lax.fori_loop(0, groups, gather_halo, 0)

        def summed(first_group, last_group, count, first):
            names = first + lax.broadcasted_iota(jnp.int32, (count, LANES), 0)

            def body(g, acc):
                at = pl.multiple_of(g * ROWS, ROWS)
                parts = []
                for j in range(ROWS):
                    mask = blk[pl.ds(at + j, 1), :] == names
                    parts.append(
                        jnp.concatenate(
                            [
                                jnp.where(mask, hi[pl.ds(at + j, 1), :], 0.0),
                                jnp.where(mask, lo[pl.ds(at + j, 1), :], 0.0),
                            ],
                            axis=0,
                        ).astype(jnp.bfloat16)
                    )
                left = jnp.concatenate(parts, axis=1)
                right = hot[:, pl.ds(pl.multiple_of(at * LANES, LANES), ROWS * LANES)]
                return acc + lax.dot_general(
                    left, right, (((1,), (1,)), ((), ())), preferred_element_type=f32
                )

            acc = lax.fori_loop(
                first_group, last_group, body, jnp.zeros((2 * count, LANES), f32)
            )
            return acc[:count] + acc[count:]

        halo_sum = summed(groups, 3 * groups, halo, own)
        for o in range(offsets):
            bwd_out[t, o] = halo_sum[o * slots : (o + 1) * slots]
        for o in range(offsets):
            when_there(shifts[o], lambda o=o: bwd_copy(t, o).start())
        total = summed(0, 3 * groups, own, 0)
        for o in range(offsets):
            when_there(-shifts[o], lambda o=o: bwd_copy(t, o).wait_recv())
        names = lax.broadcasted_iota(jnp.int32, (own, LANES), 0)
        for o in range(offsets):
            for s in range(slots):
                total = total + jnp.where(
                    names == send[0, o, s], bwd_in[t, o, s : s + 1, :], 0.0
                )
        return total

    small = lax.broadcasted_iota(jnp.int32, (1, LANES), 1)

    def whole(a):
        return jnp.sum(jnp.sum(a, axis=0, keepdims=True), axis=1, keepdims=True)

    def start_sum(k, terms):
        line = jnp.zeros((1, LANES), f32)
        for i, term in enumerate(terms):
            line = jnp.where(small == i, whole(term), line)
        sum_out[k] = line
        sum_in[k, me] = line

        def push(i, carry):
            pltpu.make_async_remote_copy(
                src_ref=sum_out.at[k],
                dst_ref=sum_in.at[k, me],
                send_sem=sum_send_sem.at[k],
                recv_sem=sum_recv_sem.at[k],
                device_id=(lax.rem(me + i, n),),
                device_id_type=pl.DeviceIdType.MESH,
            ).start()
            return carry

        lax.fori_loop(1, n, push, 0)

    def sum_bytes(k):
        return sum_in.at[k, pl.ds(0, n - 1)]

    def finish_sum(k, count):
        pltpu.make_async_copy(sum_bytes(k), sum_bytes(k), sum_recv_sem.at[k]).wait()
        line = jnp.sum(sum_in[k], axis=0)
        return [
            jnp.sum(jnp.where(small == i, line, 0.0), axis=1, keepdims=True)
            for i in range(count)
        ]

    first_residual = forcing[...] - operate(0, guess)
    field[0] = first_residual
    pack(1, field.at[0])
    start_forward(1)
    image = operate(1, field.at[0])
    field[1] = image
    pack(2, field.at[1])
    start_forward(2)
    start_sum(0, [first_residual * first_residual, first_residual * image])
    image_two = operate(2, field.at[1])
    norm, crossed = finish_sum(0, 2)
    step = norm / crossed
    first_residual = field[0]
    image = field[1]
    second = first_residual - step * image
    applied = image - step * image_two
    start_sum(1, [second * second, second * applied, second * image, first_residual * applied])
    for t in range(3):
        for o in range(offsets):
            when_there(-shifts[o], lambda t=t, o=o: fwd_copy(t, o).wait_send())
            when_there(shifts[o], lambda t=t, o=o: bwd_copy(t, o).wait_send())
    fresh, own_pair, left_pair, right_pair = finish_sum(1, 4)
    beta = fresh / norm
    next_step = fresh / (own_pair + beta * (left_pair + right_pair) + beta * beta * crossed)
    elevation[...] = (
        guess[...] + step * first_residual + next_step * (second + beta * first_residual)
    )
    residual[...] = second - next_step * (applied + beta * image)
    for k in range(2):
        pltpu.make_async_copy(sum_bytes(k), sum_bytes(k), sum_send_sem.at[k]).wait()


def local(
    n,
    forcing,
    first_guess,
    corners,
    gradients,
    element_area,
    element_depth,
    send_blocks,
    recv_blocks,
):
    own, columns = forcing.shape
    _, offsets, slots = send_blocks.shape
    count = element_area.shape[0]
    rows = count // LANES
    assert columns == LANES and own + offsets * slots <= LANES and rows % ROWS == 0
    f32 = jnp.float32
    vmem = pl.BlockSpec(memory_space=pltpu.VMEM)
    smem = pl.BlockSpec(memory_space=pltpu.SMEM)
    dma = pltpu.SemaphoreType.DMA
    part = (3, offsets, slots, LANES)
    return pl.pallas_call(
        functools.partial(kernel, n),
        out_shape=(jax.ShapeDtypeStruct((own, columns), f32),) * 2,
        in_specs=[vmem] * 6 + [smem] * 2,
        out_specs=(vmem, vmem),
        scratch_shapes=[
            pltpu.VMEM((3 * rows, LANES), jnp.int32),
            pltpu.VMEM((3 * rows, LANES), jnp.int32),
            pltpu.VMEM((LANES, 3 * count), jnp.bfloat16),
            pltpu.VMEM((4 * rows, LANES), f32),
            pltpu.VMEM((3 * rows, LANES), f32),
            pltpu.VMEM((3 * rows, LANES), f32),
            pltpu.VMEM((3 * rows, LANES), f32),
            pltpu.VMEM((2, own, LANES), f32),
            pltpu.VMEM((offsets * slots, LANES), f32),
            pltpu.VMEM(part, f32),
            pltpu.VMEM(part, f32),
            pltpu.VMEM(part, f32),
            pltpu.VMEM(part, f32),
            pltpu.VMEM((2, 1, LANES), f32),
            pltpu.VMEM((2, n, 1, LANES), f32),
            dma((3, offsets)),
            dma((3, offsets)),
            dma((3, offsets)),
            dma((3, offsets)),
            dma((2,)),
            dma((2,)),
        ],
        compiler_params=pltpu.CompilerParams(collective_id=0, has_side_effects=True),
    )(
        forcing,
        first_guess,
        corners,
        gradients,
        element_area.reshape(rows, LANES),
        element_depth.reshape(rows, LANES),
        send_blocks,
        recv_blocks,
    )


def solution(mesh):
    placed = (
        P("dom", None),
        P("dom", None),
        P(None, "dom"),
        P(None, "dom"),
        P("dom"),
        P("dom"),
        P("dom", None, None),
        P("dom", None, None),
    )
    return jax.shard_map(
        functools.partial(local, mesh.shape["dom"]),
        mesh=mesh,
        in_specs=placed,
        out_specs=(P("dom", None), P("dom", None)),
        check_vma=False,
    )
```

time: 1130 us -> 58.3 us (0.05)
  other arithmetic: 515 us -> 0 us
  local copies, waits for them, and re-layouts: 414 us -> 1.94 us
  blocking collectives: 91.1 us -> 0 us
  starting transfers between devices: 78.7 us -> 0 us
  Pallas kernels: 0 us -> 55.5 us
  waiting for transfers between devices: 14.9 us -> 0 us
    scatter-add x4 -> x0, other arithmetic: 514 us -> none  [the longest x3 385 us: operate(): jax.ops.segment_sum(contrib, flat_corners, num_segments=local_total)]
    gather x9 -> x0, local copies, waits for them, and re-layouts: 410 us -> none  [operate(): jnp.take(local_vals, corners[corner_at], axis=0)]
    psum x2 -> x0, blocking collectives: 91.1 us -> none  [paired(): lax.psum((jnp.sum(vector * vector), jnp.sum(vector * applied)), 'dom')]
    ppermute x28 -> x0, starting transfers between devices: 78.7 us -> none  [passed_along(): return lax.ppermute(block, axis, route)]
    pallas_call x0 -> x1, Pallas kernels: none -> 55.5 us  [local(): pl.pallas_call(functools.partial(kernel, n), out_shape=(jax.ShapeDtypeStr...]
    ppermute x28 -> x0, waiting for transfers between devices: 14.9 us -> none  [passed_along(): return lax.ppermute(block, axis, route)]
  transfers between devices with their start and end apart: 28 -> 0, of which waited for: 5 -> 0; matrix products, arithmetic and copies ran while one was open for 12% -> 0% of each run, Pallas kernels for 0% -> 0%
where the time goes in v1:
time: 58.3 us; the launch traced here: 58.1 us
  Pallas kernels  55.5 us (95%)
  local copies, waits for them, and re-layouts  1.94 us (3%)
  between operations  0.65 us (1%)
    pallas_call x1, Pallas kernels, local(): pl.pallas_call(functools.partial(kernel, n), out_shape=(jax.ShapeDtypeStr...  55.5 us
    unnamed x4, local copies, waits for them, and re-layouts  1.94 us

profile of v1, /device:TPU:0, one launch (start us, length us, event | category | flops | bytes accessed | tf_op | source)
XLA Modules:
  0.0 58.1 jit_solution(1633345324892711621)
XLA Ops:
  0.6 55.5 %shard_map.95 = (f32[32,128]{1,0:T(8,128)}, f32[32,128]{1,0:T(8,128)}) custom-call(f32[32,128]{1,0:T(8,128)} %forcing.1, f32[32,128]{1,0:T(8,128)} %guess.1, s32[3,8192]{1,0:T(4,128)} %corners.1, f32[4,8192]{1,0:T(4,128)} %gradients.1, f32[64,128]{1,0:T(8,128)} %bitcast.2, f32[64,128]{1,0:T(8,128)} %bitcast.3, s32[1,4,8]{2,1,0:T(4,128)} %send.1, s32[1,4,8]{2,1,0:T(4,128)} %recv.1), custom_call_target="tpu_custom_call" | custom-call | tf_op jit(solution)/shard_map/pallas_call | solution.py:371
  56.2 0.0 copy-start
  56.2 1.3 %copy.12 = f32[32,128]{1,0:T(8,128)} copy(f32[32,128]{1,0:T(8,128)} %get-tuple-element.4) | data formatting | bytes 32768
  57.5 0.0 copy-done
  57.5 0.6 %copy.13 = f32[32,128]{1,0:T(8,128)} copy(f32[32,128]{1,0:T(8,128)S(1)} %copy-done) | data formatting | bytes 32768
Async XLA Ops:
  56.2 1.3 %copy-start = (f32[32,128]{1,0:T(8,128)S(1)}, f32[32,128]{1,0:T(8,128)}, u32[]{:S(2)}) copy-start(f32[32,128]{1,0:T(8,128)} %get-tuple-element.5) | copy-start | bytes 49156

commit v2 on v1

--- a/solution.py
+++ b/solution.py
@@ -9,6 +9,7 @@
 
 LANES = 128
 ROWS = 8
+WIDE = 4
 
 
 def shift_list(offsets):
@@ -17,6 +18,14 @@
         shift_at - half_count if shift_at < half_count else shift_at - half_count + 1
         for shift_at in range(offsets)
     ]
+
+
+def learning_rounds(n, reach):
+    rounds = []
+    while reach < n - 1:
+        rounds.append(reach)
+        reach *= 2
+    return rounds
 
 
 def kernel(
@@ -52,6 +61,7 @@
     bwd_recv_sem,
     sum_send_sem,
     sum_recv_sem,
+    known,
 ):
     own, _ = forcing.shape
     _, offsets, slots = send.shape
@@ -62,16 +72,6 @@
     me = lax.axis_index("dom")
     f32 = jnp.float32
 
-    barrier = pltpu.get_barrier_semaphore()
-
-    def greet(i, carry):
-        pl.semaphore_signal(
-            barrier, inc=1, device_id=(lax.rem(me + i, n),), device_id_type=pl.DeviceIdType.MESH
-        )
-        return carry
-
-    lax.fori_loop(1, n, greet, 0)
-
     def there(distance):
         return jnp.logical_and(me + distance >= 0, me + distance < n)
 
@@ -100,6 +100,48 @@
         def _():
             action()
 
+    barrier = pltpu.get_barrier_semaphore()
+    reach = max(shifts)
+    near = [shift for shift in range(-reach, reach + 1) if shift != 0]
+    for shift in near:
+        when_there(
+            shift,
+            lambda shift=shift: pl.semaphore_signal(
+                barrier,
+                inc=1,
+                device_id=(me + shift,),
+                device_id_type=pl.DeviceIdType.MESH,
+            ),
+        )
+
+    rounds = learning_rounds(n, reach)
+
+    def tell(i):
+        for side in range(2):
+            far = rounds[i] * (2 * side - 1)
+            when_there(
+                far,
+                lambda side=side, far=far: pl.semaphore_signal(
+                    known.at[i, side],
+                    inc=1,
+                    device_id=(me + far,),
+                    device_id_type=pl.DeviceIdType.MESH,
+                ),
+            )
+
+    def learn(i):
+        for side in range(2):
+            far = rounds[i] * (1 - 2 * side)
+            when_there(
+                far, lambda side=side: pl.semaphore_wait(known.at[i, side], 1)
+            )
+
+    def next_round(i):
+        if i > 0 and i <= len(rounds):
+            learn(i - 1)
+        if i < len(rounds):
+            tell(i)
+
     for o in range(offsets):
 
         @pl.when(jnp.logical_not(there(shifts[o])))
@@ -121,10 +163,6 @@
     def start_forward(t):
         for o in range(offsets):
             when_there(-shifts[o], lambda o=o: fwd_copy(t, o).start())
-
-    pack(0, guess)
-    pl.semaphore_wait(barrier, n - 1)
-    start_forward(0)
 
     def lay(r, carry):
         at = pl.multiple_of(r * LANES, LANES)
@@ -161,12 +199,20 @@
         at = pl.multiple_of(g * ROWS, ROWS)
         for j in range(ROWS):
             row = lane[pl.ds(at + j, 1), :]
-            hot[:, pl.ds(pl.multiple_of((at + j) * LANES, LANES), LANES)] = jnp.where(
-                row == tall, 1.0, 0.0
-            ).astype(jnp.bfloat16)
+            hot[pl.ds(pl.multiple_of((at + j) * LANES, LANES), LANES), :] = (
+                jnp.where(row == tall, 1.0, 0.0).T.astype(jnp.bfloat16)
+            )
         return carry
 
-    lax.fori_loop(0, 3 * groups, heat, 0)
+    half = 3 * groups // 2
+    lax.fori_loop(0, half, heat, 0)
+    pack(0, guess)
+    pl.semaphore_wait(
+        barrier, jnp.minimum(me, reach) + jnp.minimum(n - 1 - me, reach)
+    )
+    start_forward(0)
+    next_round(0)
+    lax.fori_loop(half, 3 * groups, heat, 0)
 
     def picked(source, count, first, value, index, block):
         for b in range(count):
@@ -175,27 +221,25 @@
             value = jnp.where(block == first + b, got, value)
         return value
 
-    def operate(t, source):
+    def operate(t, source, between):
         def gather_own(g, carry):
-            at = pl.multiple_of(g * ROWS, ROWS)
-            index = lane[pl.ds(at, ROWS), :]
-            block = blk[pl.ds(at, ROWS), :]
-            vals[pl.ds(at, ROWS), :] = picked(
-                lambda b: source[b : b + 1, :],
-                own,
-                0,
-                jnp.zeros((ROWS, LANES), f32),
-                index,
-                block,
-            )
+            for j in range(WIDE):
+                at = pl.multiple_of((g * WIDE + j) * ROWS, ROWS)
+                vals[pl.ds(at, ROWS), :] = picked(
+                    lambda b: source[b : b + 1, :],
+                    own,
+                    0,
+                    jnp.zeros((ROWS, LANES), f32),
+                    lane[pl.ds(at, ROWS), :],
+                    blk[pl.ds(at, ROWS), :],
+                )
             return carry
 
-        lax.fori_loop(0, 3 * groups, gather_own, 0)
-
+        lax.fori_loop(0, 3 * groups // WIDE, gather_own, 0)
         for o in range(offsets):
             when_there(shifts[o], lambda o=o: fwd_copy(t, o).wait_recv())
 
-        def gather_halo(g, carry):
+        def one_group(g, energy):
             at = pl.multiple_of(g * ROWS, ROWS)
             u = [vals[pl.ds(at, ROWS), :]]
             for c in (1, 2):
@@ -231,17 +275,27 @@
                 top = adds[c].astype(jnp.bfloat16).astype(f32)
                 hi[pl.ds(here, ROWS), :] = top
                 lo[pl.ds(here, ROWS), :] = adds[c] - top
-            return carry
-
-        lax.fori_loop(0, groups, gather_halo, 0)
+            return energy + (
+                slope_x * (gx0 * from0 + gx1 * from1)
+                + slope_y * (gy0 * from0 + gy1 * from1)
+                + third * (u[0] * u[0] + u[1] * u[1] + u[2] * u[2])
+            )
+
+        def gather_halo(g, energy):
+            for j in range(2):
+                energy = one_group(g * 2 + j, energy)
+            return energy
+
+        energy = lax.fori_loop(0, groups // 2, gather_halo, jnp.zeros((ROWS, LANES), f32))
+        between(energy)
 
         def summed(first_group, last_group, count, first):
             names = first + lax.broadcasted_iota(jnp.int32, (count, LANES), 0)
 
             def body(g, acc):
-                at = pl.multiple_of(g * ROWS, ROWS)
+                at = pl.multiple_of(g * WIDE * ROWS, ROWS)
                 parts = []
-                for j in range(ROWS):
+                for j in range(WIDE * ROWS):
                     mask = blk[pl.ds(at + j, 1), :] == names
                     parts.append(
                         jnp.concatenate(
@@ -253,21 +307,23 @@
                         ).astype(jnp.bfloat16)
                     )
                 left = jnp.concatenate(parts, axis=1)
-                right = hot[:, pl.ds(pl.multiple_of(at * LANES, LANES), ROWS * LANES)]
-                return acc + lax.dot_general(
-                    left, right, (((1,), (1,)), ((), ())), preferred_element_type=f32
-                )
+                right = hot[pl.ds(pl.multiple_of(at * LANES, LANES), WIDE * ROWS * LANES), :]
+                return acc + jnp.dot(left, right, preferred_element_type=f32)
 
             acc = lax.fori_loop(
-                first_group, last_group, body, jnp.zeros((2 * count, LANES), f32)
+                first_group // WIDE, last_group // WIDE, body, jnp.zeros((2 * count, LANES), f32)
             )
             return acc[:count] + acc[count:]
 
+        if t == 0:
+            next_round(1)
         halo_sum = summed(groups, 3 * groups, halo, own)
         for o in range(offsets):
             bwd_out[t, o] = halo_sum[o * slots : (o + 1) * slots]
         for o in range(offsets):
             when_there(shifts[o], lambda o=o: bwd_copy(t, o).start())
+        if t == 0:
+            next_round(2)
         total = summed(0, 3 * groups, own, 0)
         for o in range(offsets):
             when_there(-shifts[o], lambda o=o: bwd_copy(t, o).wait_recv())
@@ -315,34 +371,38 @@
             for i in range(count)
         ]
 
-    first_residual = forcing[...] - operate(0, guess)
-    field[0] = first_residual
+    field[0] = forcing[...] - operate(0, guess, lambda energy: None)
     pack(1, field.at[0])
     start_forward(1)
-    image = operate(1, field.at[0])
-    field[1] = image
+
+    next_round(3)
+
+    def first_sums(energy):
+        for i in range(4, len(rounds) + 1):
+            next_round(i)
+        start_sum(0, [field[0] * field[0], energy])
+
+    image = operate(1, field.at[0], first_sums)
+    norm, crossed = finish_sum(0, 2)
+    step = norm / crossed
+    field[1] = field[0] - step * image
     pack(2, field.at[1])
     start_forward(2)
-    start_sum(0, [first_residual * first_residual, first_residual * image])
-    image_two = operate(2, field.at[1])
-    norm, crossed = finish_sum(0, 2)
-    step = norm / crossed
-    first_residual = field[0]
-    image = field[1]
-    second = first_residual - step * image
-    applied = image - step * image_two
-    start_sum(1, [second * second, second * applied, second * image, first_residual * applied])
+    field[2] = image
+
+    def second_sums(energy):
+        start_sum(1, [field[1] * field[1], energy, field[1] * field[2]])
+
+    applied = operate(2, field.at[1], second_sums)
     for t in range(3):
         for o in range(offsets):
             when_there(-shifts[o], lambda t=t, o=o: fwd_copy(t, o).wait_send())
             when_there(shifts[o], lambda t=t, o=o: bwd_copy(t, o).wait_send())
-    fresh, own_pair, left_pair, right_pair = finish_sum(1, 4)
+    fresh, own_pair, mixed = finish_sum(1, 3)
     beta = fresh / norm
-    next_step = fresh / (own_pair + beta * (left_pair + right_pair) + beta * beta * crossed)
-    elevation[...] = (
-        guess[...] + step * first_residual + next_step * (second + beta * first_residual)
-    )
-    residual[...] = second - next_step * (applied + beta * image)
+    next_step = fresh / (own_pair + beta * (2.0 * mixed + beta * crossed))
+    elevation[...] = guess[...] + step * field[0] + next_step * (field[1] + beta * field[0])
+    residual[...] = field[1] - next_step * (applied + beta * field[2])
     for k in range(2):
         pltpu.make_async_copy(sum_bytes(k), sum_bytes(k), sum_send_sem.at[k]).wait()
 
@@ -362,7 +422,7 @@
     _, offsets, slots = send_blocks.shape
     count = element_area.shape[0]
     rows = count // LANES
-    assert columns == LANES and own + offsets * slots <= LANES and rows % ROWS == 0
+    assert columns == LANES and own + offsets * slots <= LANES and rows % (ROWS * WIDE) == 0
     f32 = jnp.float32
     vmem = pl.BlockSpec(memory_space=pltpu.VMEM)
     smem = pl.BlockSpec(memory_space=pltpu.SMEM)
@@ -376,12 +436,12 @@
         scratch_shapes=[
             pltpu.VMEM((3 * rows, LANES), jnp.int32),
             pltpu.VMEM((3 * rows, LANES), jnp.int32),
-            pltpu.VMEM((LANES, 3 * count), jnp.bfloat16),
+            pltpu.VMEM((3 * count, LANES), jnp.bfloat16),
             pltpu.VMEM((4 * rows, LANES), f32),
             pltpu.VMEM((3 * rows, LANES), f32),
             pltpu.VMEM((3 * rows, LANES), f32),
             pltpu.VMEM((3 * rows, LANES), f32),
-            pltpu.VMEM((2, own, LANES), f32),
+            pltpu.VMEM((3, own, LANES), f32),
             pltpu.VMEM((offsets * slots, LANES), f32),
             pltpu.VMEM(part, f32),
             pltpu.VMEM(part, f32),
@@ -395,6 +455,7 @@
             dma((3, offsets)),
             dma((2,)),
             dma((2,)),
+            pltpu.SemaphoreType.REGULAR((len(learning_rounds(n, max(shift_list(offsets)))) + 1, 2)),
         ],
         compiler_params=pltpu.CompilerParams(collective_id=0, has_side_effects=True),
     )(

time: 58.3 us -> 40 us (0.69)
  Pallas kernels: 55.5 us -> 37.2 us
    pallas_call x1, Pallas kernels: 55.5 us -> 37.2 us  [local(): pl.pallas_call(functools.partial(kernel, n), out_shape=(jax.ShapeDtypeStr...]
where the time goes in v2:
time: 40 us; the launch traced here: 39.8 us
  Pallas kernels  37.2 us (93%)
  local copies, waits for them, and re-layouts  1.94 us (5%)
  between operations  0.65 us (2%)
    pallas_call x1, Pallas kernels, local(): pl.pallas_call(functools.partial(kernel, n), out_shape=(jax.ShapeDtypeStr...  37.2 us
    unnamed x4, local copies, waits for them, and re-layouts  1.94 us

profile of v2, /device:TPU:0, one launch (start us, length us, event | category | flops | bytes accessed | tf_op | source)
XLA Modules:
  0.0 39.8 jit_solution(18238036391117959373)
XLA Ops:
  0.6 37.2 %shard_map.95 = (f32[32,128]{1,0:T(8,128)}, f32[32,128]{1,0:T(8,128)}) custom-call(f32[32,128]{1,0:T(8,128)} %forcing.1, f32[32,128]{1,0:T(8,128)} %guess.1, s32[3,8192]{1,0:T(4,128)} %corners.1, f32[4,8192]{1,0:T(4,128)} %gradients.1, f32[64,128]{1,0:T(8,128)} %bitcast.2, f32[64,128]{1,0:T(8,128)} %bitcast.3, s32[1,4,8]{2,1,0:T(4,128)} %send.1, s32[1,4,8]{2,1,0:T(4,128)} %recv.1), custom_call_target="tpu_custom_call" | custom-call | tf_op jit(solution)/shard_map/pallas_call | solution.py:431
  37.9 0.0 copy-start
  37.9 1.3 %copy.12 = f32[32,128]{1,0:T(8,128)} copy(f32[32,128]{1,0:T(8,128)} %get-tuple-element.4) | data formatting | bytes 32768
  39.2 0.0 copy-done
  39.2 0.6 %copy.13 = f32[32,128]{1,0:T(8,128)} copy(f32[32,128]{1,0:T(8,128)S(1)} %copy-done) | data formatting | bytes 32768
Async XLA Ops:
  37.9 1.3 %copy-start = (f32[32,128]{1,0:T(8,128)S(1)}, f32[32,128]{1,0:T(8,128)}, u32[]{:S(2)}) copy-start(f32[32,128]{1,0:T(8,128)} %get-tuple-element.5) | copy-start | bytes 49156

commit v3 on v2

--- a/solution.py
+++ b/solution.py
@@ -38,8 +38,7 @@
     depth,
     send,
     recv,
-    elevation,
-    residual,
+    both,
     blk,
     lane,
     hot,
@@ -204,15 +203,14 @@
             )
         return carry
 
-    half = 3 * groups // 2
-    lax.fori_loop(0, half, heat, 0)
+    lax.fori_loop(groups, 2 * groups, heat, 0)
     pack(0, guess)
     pl.semaphore_wait(
         barrier, jnp.minimum(me, reach) + jnp.minimum(n - 1 - me, reach)
     )
     start_forward(0)
     next_round(0)
-    lax.fori_loop(half, 3 * groups, heat, 0)
+    lax.fori_loop(2 * groups, 3 * groups, heat, 0)
 
     def picked(source, count, first, value, index, block):
         for b in range(count):
@@ -221,11 +219,11 @@
             value = jnp.where(block == first + b, got, value)
         return value
 
-    def operate(t, source, between):
+    def operate(t, source, between, after, finished):
         def gather_own(g, carry):
             for j in range(WIDE):
                 at = pl.multiple_of((g * WIDE + j) * ROWS, ROWS)
-                vals[pl.ds(at, ROWS), :] = picked(
+                vals[t // 2, pl.ds(at, ROWS), :] = picked(
                     lambda b: source[b : b + 1, :],
                     own,
                     0,
@@ -239,9 +237,11 @@
         for o in range(offsets):
             when_there(shifts[o], lambda o=o: fwd_copy(t, o).wait_recv())
 
+        step = finished()
+
         def one_group(g, energy):
             at = pl.multiple_of(g * ROWS, ROWS)
-            u = [vals[pl.ds(at, ROWS), :]]
+            u = [vals[t // 2, pl.ds(at, ROWS), :]]
             for c in (1, 2):
                 here = pl.multiple_of(c * rows + at, ROWS)
                 u.append(
@@ -249,11 +249,17 @@
                         lambda b: fwd_in[t, b // slots, b % slots : b % slots + 1, :],
                         halo,
                         own,
-                        vals[pl.ds(here, ROWS), :],
+                        vals[t // 2, pl.ds(here, ROWS), :],
                         lane[pl.ds(here, ROWS), :],
                         blk[pl.ds(here, ROWS), :],
                     )
                 )
+                if t == 1:
+                    vals[0, pl.ds(here, ROWS), :] = u[c]
+            if t == 2:
+                for c in range(3):
+                    here = pl.multiple_of(c * rows + at, ROWS)
+                    u[c] = vals[0, pl.ds(here, ROWS), :] - step * u[c]
             gx0, gy0, gx1, gy1 = [
                 elem[pl.ds(pl.multiple_of(c * rows + at, ROWS), ROWS), :] for c in range(4)
             ]
@@ -322,8 +328,10 @@
             bwd_out[t, o] = halo_sum[o * slots : (o + 1) * slots]
         for o in range(offsets):
             when_there(shifts[o], lambda o=o: bwd_copy(t, o).start())
+        after()
         if t == 0:
             next_round(2)
+            lax.fori_loop(0, groups, heat, 0)
         total = summed(0, 3 * groups, own, 0)
         for o in range(offsets):
             when_there(-shifts[o], lambda o=o: bwd_copy(t, o).wait_recv())
@@ -371,29 +379,37 @@
             for i in range(count)
         ]
 
-    field[0] = forcing[...] - operate(0, guess, lambda energy: None)
+    def nothing(*_):
+        return None
+
+    field[0] = forcing[...] - operate(0, guess, nothing, nothing, nothing)
     pack(1, field.at[0])
     start_forward(1)
-
     next_round(3)
-
-    def first_sums(energy):
-        for i in range(4, len(rounds) + 1):
-            next_round(i)
-        start_sum(0, [field[0] * field[0], energy])
-
-    image = operate(1, field.at[0], first_sums)
-    norm, crossed = finish_sum(0, 2)
-    step = norm / crossed
-    field[1] = field[0] - step * image
-    pack(2, field.at[1])
+    for i in range(4, len(rounds) + 1):
+        next_round(i)
+    energies = []
+
+    def first_sums():
+        start_sum(0, [field[0] * field[0], energies[0]])
+
+    field[2] = operate(1, field.at[0], energies.append, first_sums, nothing)
+    pack(2, field.at[2])
     start_forward(2)
-    field[2] = image
+    sums = []
+
+    def first_step():
+        norm, crossed = finish_sum(0, 2)
+        step = norm / crossed
+        sums.extend([norm, crossed, step])
+        field[1] = field[0] - step * field[2]
+        return step
 
     def second_sums(energy):
         start_sum(1, [field[1] * field[1], energy, field[1] * field[2]])
 
-    applied = operate(2, field.at[1], second_sums)
+    applied = operate(2, field.at[2], second_sums, nothing, first_step)
+    norm, crossed, step = sums
     for t in range(3):
         for o in range(offsets):
             when_there(-shifts[o], lambda t=t, o=o: fwd_copy(t, o).wait_send())
@@ -401,8 +417,8 @@
     fresh, own_pair, mixed = finish_sum(1, 3)
     beta = fresh / norm
     next_step = fresh / (own_pair + beta * (2.0 * mixed + beta * crossed))
-    elevation[...] = guess[...] + step * field[0] + next_step * (field[1] + beta * field[0])
-    residual[...] = field[1] - next_step * (applied + beta * field[2])
+    both[0:own] = guess[...] + step * field[0] + next_step * (field[1] + beta * field[0])
+    both[own : 2 * own] = field[1] - next_step * (applied + beta * field[2])
     for k in range(2):
         pltpu.make_async_copy(sum_bytes(k), sum_bytes(k), sum_send_sem.at[k]).wait()
 
@@ -428,17 +444,17 @@
     smem = pl.BlockSpec(memory_space=pltpu.SMEM)
     dma = pltpu.SemaphoreType.DMA
     part = (3, offsets, slots, LANES)
-    return pl.pallas_call(
+    both = pl.pallas_call(
         functools.partial(kernel, n),
-        out_shape=(jax.ShapeDtypeStruct((own, columns), f32),) * 2,
+        out_shape=jax.ShapeDtypeStruct((2 * own, columns), f32),
         in_specs=[vmem] * 6 + [smem] * 2,
-        out_specs=(vmem, vmem),
+        out_specs=vmem,
         scratch_shapes=[
             pltpu.VMEM((3 * rows, LANES), jnp.int32),
             pltpu.VMEM((3 * rows, LANES), jnp.int32),
             pltpu.VMEM((3 * count, LANES), jnp.bfloat16),
             pltpu.VMEM((4 * rows, LANES), f32),
-            pltpu.VMEM((3 * rows, LANES), f32),
+            pltpu.VMEM((2, 3 * rows, LANES), f32),
             pltpu.VMEM((3 * rows, LANES), f32),
             pltpu.VMEM((3 * rows, LANES), f32),
             pltpu.VMEM((3, own, LANES), f32),
@@ -468,6 +484,7 @@
         send_blocks,
         recv_blocks,
     )
+    return both[:own], both[own:]
 
 
 def solution(mesh):

time: 40 us -> 38.5 us (0.963)
  Pallas kernels: 37.2 us -> 36.3 us
  local copies, waits for them, and re-layouts: 1.94 us -> 1.35 us
    unnamed x4 -> x0, local copies, waits for them, and re-layouts: 1.94 us -> none
    slice x0 -> x1, local copies, waits for them, and re-layouts: none -> 1.35 us  [local(): return (both[:own], both[own:])]
    pallas_call x1, Pallas kernels: 37.2 us -> 36.3 us  [local(): pl.pallas_call(functools.partial(kernel, n), out_shape=jax.ShapeDtypeStru...]
where the time goes in v3:
time: 38.5 us; the launch traced here: 38.3 us
  Pallas kernels  36.3 us (94%)
  local copies, waits for them, and re-layouts  1.35 us (4%)
  between operations  0.64 us (2%)
    pallas_call x1, Pallas kernels, local(): pl.pallas_call(functools.partial(kernel, n), out_shape=jax.ShapeDtypeStru...  36.3 us
    slice x1, local copies, waits for them, and re-layouts, local(): return (both[:own], both[own:])  1.35 us

profile of v3, /device:TPU:0, one launch (start us, length us, event | category | flops | bytes accessed | tf_op | source)
XLA Modules:
  0.0 38.3 jit_solution(17457225126419254873)
XLA Ops:
  0.6 36.3 %shard_map.95 = f32[64,128]{1,0:T(8,128)} custom-call(f32[32,128]{1,0:T(8,128)} %forcing.1, f32[32,128]{1,0:T(8,128)} %guess.1, s32[3,8192]{1,0:T(4,128)} %corners.1, f32[4,8192]{1,0:T(4,128)} %gradients.1, f32[64,128]{1,0:T(8,128)} %bitcast.2, f32[64,128]{1,0:T(8,128)} %bitcast.3, s32[1,4,8]{2,1,0:T(4,128)} %send.1, s32[1,4,8]{2,1,0:T(4,128)} %recv.1), custom_call_target="tpu_custom_call" | custom-call | tf_op jit(solution)/shard_map/pallas_call | solution.py:447
  36.9 1.3 %fusion = (f32[32,128]{1,0:T(8,128)}, f32[32,128]{1,0:T(8,128)}) fusion(f32[64,128]{1,0:T(8,128)} %shard_map.95), kind=kLoop, calls=%fused_computation | loop fusion | bytes 65536 | tf_op jit(solution)/shard_map/slice | solution.py:487
